TPU v7x, 32 devices: a whole 2x2x4 slice. The times are simulated.
32 devices in a mesh: loc: 32 (over z, y, x, core).
Axes of the slice: x: 2, y: 2, z: 4, core: 2. Of those that a mesh axis runs over, the one named last changes fastest.
Arguments:
- hazard_bins: int32 [256, 8192], P(None, 'loc'), may hold values from 0 to 63
- curve_index: int32 [8192], P('loc'), may hold values from 0 to 255
- damage_table: float32 [256, 64], replicated, may hold values from 0.02 to 0.9
- insured_value: float32 [8192], P('loc'), may hold values from 0.5 to 5
- deductible: float32 [8192], P('loc'), may hold values from 0.05 to 0.5
- loss_limit: float32 [8192], P('loc'), may hold values from 0.5 to 3
- uncertainty: float32 [128, 8192], P(None, 'loc'), may hold values from 0.5 to 2
- year_ids: int32 [256], replicated, may hold values from 0 to 63
Outputs:
- event_loss: float32 [256, 128], P('loc')
- year_loss: float32 [64, 128], replicated
All inputs are finite; a program needn't handle non-finite values.
Results may differ from a plain program's by a relative error of at most 0.00005.
Values sent between devices are 32-bit elements; how exact they have to be, the bound alone decides.
A program may use at most 64 MiB of HBM per device.

v0:
```python
import math
import jax
import jax.numpy as jnp
from jax import lax
from jax.sharding import PartitionSpec as P

YEARS = 64


def shards(
    hazard_bins,
    curve_index,
    damage_table,
    insured_value,
    deductible,
    loss_limit,
    uncertainty,
    year_ids,
):
    curve_count = damage_table.shape[0]
    bin_count = damage_table.shape[1]
    selector = (curve_index[None, :] == jnp.arange(curve_count, dtype=jnp.int32)[:, None]).astype(
        jnp.float32
    )
    curve_rows = jnp.dot(
        damage_table.T,
        selector,
        precision=lax.Precision.HIGHEST,
        preferred_element_type=jnp.float32,
    )
    bin_ids = jnp.arange(bin_count, dtype=jnp.int32)[None, :, None]
    shard_width = insured_value.shape[0]
    locations = shard_width * lax.axis_size("loc")
    event_total = hazard_bins.shape[0]
    own_rows = event_total // lax.axis_size("loc")
    year_range = jnp.arange(YEARS, dtype=jnp.int32)
    target_rows = max(16, 32768 // shard_width)
    target_rows = 1 << target_rows.bit_length() - 1

    def block_terms(hazard_block):
        ratios = jnp.sum(
            jnp.where(hazard_block[:, None, :] == bin_ids, curve_rows[None, :, :], 0.0), axis=1
        )
        damage = jnp.minimum(ratios[:, None, :] * uncertainty[None, :, :], 1.0)
        losses = jnp.minimum(jnp.maximum(insured_value * damage - deductible, 0.0), loss_limit)
        return jnp.sum(losses, axis=2)

    block_rows = math.gcd(event_total, target_rows)
    grouped = hazard_bins.reshape(event_total // block_rows, block_rows, hazard_bins.shape[1])
    summed = lax.psum(
        lax.map(block_terms, grouped).reshape(event_total, uncertainty.shape[0]), "loc"
    )
    all_events = summed * (1.0 / locations)
    membership = (year_ids[:, None] == year_range[None, :]).astype(jnp.float32)
    year_loss = jnp.dot(
        membership.T,
        all_events,
        precision=lax.Precision.HIGHEST,
        preferred_element_type=jnp.float32,
    ) * (YEARS / event_total)
    event_loss = lax.dynamic_slice_in_dim(all_events, lax.axis_index("loc") * own_rows, own_rows, 0)
    return (event_loss, year_loss)


def solution(mesh):
    return jax.shard_map(
        shards,
        mesh=mesh,
        in_specs=(P(None, "loc"), P("loc"), P(), P("loc"), P("loc"), P("loc"), P(None, "loc"), P()),
        out_specs=(P("loc", None), P()),
        check_vma=False,
    )
```

profile of v0, /device:TPU:0, one launch (start us, length us, event | category | flops | bytes accessed | tf_op | source)
XLA Modules:
  0.0 161.2 jit_solution(17336315742773112577)
XLA Ops:
  7.2 0.0 copy-start
  7.2 0.0 all-reduce.2.cloned.1.call-start
  7.2 0.8 copy-done
  8.0 0.9 convolution_bitcast_fusion
  8.9 14.9 %while.11 = (s32[]{:T(128)}, f32[2,128,128]{2,1,0:T(8,128)S(1)}, f32[256]{0:T(256)}, s32[2,128,256]{2,1,0:T(8,128)}, f32[64,256]{1,0:T(8,128)S(1)}, /*index=5*/f...) while((s32[]{:T(128)}, f32[2,128,128]{2,1,0:T(8,128)S(1)}, f32[256]{0:T(256)}, ...), condition=%wide.region_3.4_spmd.clone, body=%wide.region_0.3_spmd.clone.sunk | while | flops 35602432 | bytes 1588437 | solution.py:51
  8.9 0.0 copy-start.1
  8.9 0.0 copy-start.4
  9.0 0.0 copy-start.5
  9.0 0.0 copy-start.6
  9.0 1.0 dynamic-slice_bitcast_fusion.2
  10.0 2.4 %select_reduce_fusion.2 = f32[128,256]{1,0:T(8,128)S(1)} fusion(f32[64,256]{1,0:T(8,128)S(1)} %get-tuple-element.155, s32[128,256]{1,0:T(8,128)S(1)} %dynamic-slice_bitcast_fusion.2), kind=kLoop, calls=%fused_computation.3.clone.1 | loop fusion | flops 6258688 | bytes 327680 | tf_op jit(solution)/shard_map/while/body/eval_jaxpr/reduce_sum | solution.py:41
  12.4 0.0 copy-done.1
  12.4 0.0 copy-done.4
  12.4 0.0 copy-done.5
  12.4 0.0 copy-done.6
  12.4 3.9 %minimum_reduce_fusion.2 = f32[128,128]{1,0:T(8,128)S(1)} fusion(f32[256]{0:T(256)S(1)} %copy-done.6, f32[256]{0:T(256)S(1)} %copy-done.5, f32[128,256]{1,0:T(8,128)S(1)} %copy-done.1, f32[128,256]{1,0:T(8,128)S(1)} %select_reduce_fusion.2, f32[256]{0:T(256)S(1)} %copy-done.4), kind=kLoop, calls=%fused_computation.1.clone.1 | loop fusion | flops 29343744 | bytes 330752 | tf_op jit(solution)/shard_map/while/body/eval_jaxpr/reduce_sum | solution.py:46
  16.4 0.0 copy-start.1
  16.4 0.0 copy-start.4
  16.4 0.0 copy-start.5
  16.4 0.0 copy-start.6
  16.4 1.0 dynamic-slice_bitcast_fusion.2
  17.4 2.4 %select_reduce_fusion.2 = f32[128,256]{1,0:T(8,128)S(1)} fusion(f32[64,256]{1,0:T(8,128)S(1)} %get-tuple-element.155, s32[128,256]{1,0:T(8,128)S(1)} %dynamic-slice_bitcast_fusion.2), kind=kLoop, calls=%fused_computation.3.clone.1 | loop fusion | flops 6258688 | bytes 327680 | tf_op jit(solution)/shard_map/while/body/eval_jaxpr/reduce_sum | solution.py:41
  19.8 0.0 copy-done.1
  19.8 0.0 copy-done.4
  19.8 0.0 copy-done.5
  19.8 0.0 copy-done.6
  19.8 3.9 %minimum_reduce_fusion.2 = f32[128,128]{1,0:T(8,128)S(1)} fusion(f32[256]{0:T(256)S(1)} %copy-done.6, f32[256]{0:T(256)S(1)} %copy-done.5, f32[128,256]{1,0:T(8,128)S(1)} %copy-done.1, f32[128,256]{1,0:T(8,128)S(1)} %select_reduce_fusion.2, f32[256]{0:T(256)S(1)} %copy-done.4), kind=kLoop, calls=%fused_computation.1.clone.1 | loop fusion | flops 29343744 | bytes 330752 | tf_op jit(solution)/shard_map/while/body/eval_jaxpr/reduce_sum | solution.py:46
  23.8 0.0 copy-start.3
  23.8 0.0 copy-start.7
  23.8 0.6 copy-done.3
  24.4 0.0 all-reduce.2.cloned.1.call-update
  24.4 127.3 %all-reduce.2.cloned.1.call-done = f32[256,128]{1,0:T(8,128)} async-done(((f32[256,128]{1,0:T(8,128)}), f32[256,128]{1,0:T(8,128)}) %all-reduce.2.cloned.1.call-update) | async-done | bytes 131088 | tf_op jit(solution)/shard_map/psum | solution.py:50
  151.8 0.0 copy-start.2
  151.8 1.0 broadcast_multiply_fusion
  152.8 0.6 constant_dynamic-slice_fusion
  153.4 0.0 copy-done.7
  153.4 0.0 copy-done.2
  153.4 1.0 convolution_multiply_fusion
  (3 shorter events, 0.0 us)
Async XLA Ops:
  7.2 0.8 copy-start
  7.2 144.6 %all-reduce.2.cloned.1.call-start = ((), (), s32[]{:S(2)}) async-start(), calls=%async_computation | async-start | bytes 262144 | tf_op jit(solution)/shard_map/psum | solution.py:50
  8.9 3.4 %copy-start.1 = (f32[128,256]{1,0:T(8,128)S(1)}, f32[128,256]{1,0:T(8,128)}, u32[]{:S(2)}) copy-start(f32[128,256]{1,0:T(8,128)} %get-tuple-element.156) | copy-start | bytes 393220 | tf_op jit(solution)/shard_map/while
  8.9 3.4 %copy-start.4 = (f32[256]{0:T(256)S(1)}, f32[256]{0:T(256)}, u32[]{:S(2)}) copy-start(f32[256]{0:T(256)} %get-tuple-element.153) | copy-start | bytes 3076 | tf_op jit(solution)/shard_map/while
  9.0 3.4 %copy-start.5 = (f32[256]{0:T(256)S(1)}, f32[256]{0:T(256)}, u32[]{:S(2)}) copy-start(f32[256]{0:T(256)} %get-tuple-element.157) | copy-start | bytes 3076 | tf_op jit(solution)/shard_map/while
  9.0 3.4 %copy-start.6 = (f32[256]{0:T(256)S(1)}, f32[256]{0:T(256)}, u32[]{:S(2)}) copy-start(f32[256]{0:T(256)} %get-tuple-element.158) | copy-start | bytes 3076 | tf_op jit(solution)/shard_map/while
  16.4 3.4 %copy-start.1 = (f32[128,256]{1,0:T(8,128)S(1)}, f32[128,256]{1,0:T(8,128)}, u32[]{:S(2)}) copy-start(f32[128,256]{1,0:T(8,128)} %get-tuple-element.156) | copy-start | bytes 393220 | tf_op jit(solution)/shard_map/while
  16.4 3.4 %copy-start.4 = (f32[256]{0:T(256)S(1)}, f32[256]{0:T(256)}, u32[]{:S(2)}) copy-start(f32[256]{0:T(256)} %get-tuple-element.153) | copy-start | bytes 3076 | tf_op jit(solution)/shard_map/while
  16.4 3.4 %copy-start.5 = (f32[256]{0:T(256)S(1)}, f32[256]{0:T(256)}, u32[]{:S(2)}) copy-start(f32[256]{0:T(256)} %get-tuple-element.157) | copy-start | bytes 3076 | tf_op jit(solution)/shard_map/while
  16.4 3.4 %copy-start.6 = (f32[256]{0:T(256)S(1)}, f32[256]{0:T(256)}, u32[]{:S(2)}) copy-start(f32[256]{0:T(256)} %get-tuple-element.158) | copy-start | bytes 3076 | tf_op jit(solution)/shard_map/while
  23.8 0.6 copy-start.3
  23.8 129.6 %copy-start.7 = (s32[256]{0:T(256)S(1)}, s32[256]{0:T(256)}, u32[]{:S(2)}) copy-start(s32[256]{0:T(256)} %param.17) | copy-start | bytes 3076
  151.8 1.6 copy-start.2
Sparse Core Ops, SparseCore 0:
  24.6 127.1 all-reduce.1
where the time goes:
time: 161 us
  waiting for transfers between devices  127 us (79%)
  between operations  14.1 us (9%)
  other arithmetic  13.6 us (8%)
  local copies, waits for them, and re-layouts  4.04 us (3%)
  matrix products  1.85 us (1%)
    psum x1, waiting for transfers between devices, shards(): lax.psum(lax.map(block_terms, grouped).reshape(event_total, uncertainty.s...  127 us
    reduce_sum x2, other arithmetic, block_terms(): return jnp.sum(losses, axis=2)  7.85 us
    reduce_sum x2, other arithmetic, block_terms(): jnp.sum(jnp.where(hazard_block[:, None, :] == bin_ids, curve_rows[None, :...  4.8 us
  transfers between devices with their start and end apart: 1, of which 1 were waited for; matrix products, arithmetic and copies ran while one was open for 0% of the time, Pallas kernels for 0%

commit v1 on v0

--- a/solution.py
+++ b/solution.py
@@ -47,9 +47,8 @@
 
     block_rows = math.gcd(event_total, target_rows)
     grouped = hazard_bins.reshape(event_total // block_rows, block_rows, hazard_bins.shape[1])
-    summed = lax.psum(
-        lax.map(block_terms, grouped).reshape(event_total, uncertainty.shape[0]), "loc"
-    )
+    in_array = lax.map(block_terms, grouped).reshape(event_total, uncertainty.shape[0])
+    summed = jnp.sum(lax.all_gather(in_array, "loc"), axis=0)
     all_events = summed * (1.0 / locations)
     membership = (year_ids[:, None] == year_range[None, :]).astype(jnp.float32)
     year_loss = jnp.dot(

time: 161 us -> 102 us (0.63)
  waiting for transfers between devices: 127 us -> 64.5 us
  other arithmetic: 13.6 us -> 17 us
    psum x1 -> x0, waiting for transfers between devices: 127 us -> none  [shards(): lax.psum(lax.map(block_terms, grouped).reshape(event_total, uncertainty.s...]
    all_gather x0 -> x1, waiting for transfers between devices: none -> 64.5 us  [shards(): summed = jnp.sum(lax.all_gather(in_array, 'loc'), axis=0)]
    reduce_sum x0 -> x1, other arithmetic: none -> 2.4 us  [shards(): summed = jnp.sum(lax.all_gather(in_array, 'loc'), axis=0)]
    reduce_sum x2, other arithmetic: 7.85 us -> 9.77 us  [block_terms(): return jnp.sum(losses, axis=2)]
where the time goes in v1:
time: 102 us; the launch traced here: 101 us
  waiting for transfers between devices  64.5 us (63%)
  other arithmetic  17 us (17%)
  between operations  14.1 us (14%)
  local copies, waits for them, and re-layouts  3.88 us (4%)
  matrix products  1.85 us (2%)
    all_gather x1, waiting for transfers between devices, shards(): summed = jnp.sum(lax.all_gather(in_array, 'loc'), axis=0)  64.5 us
    reduce_sum x2, other arithmetic, block_terms(): return jnp.sum(losses, axis=2)  9.77 us
    reduce_sum x2, other arithmetic, block_terms(): jnp.sum(jnp.where(hazard_block[:, None, :] == bin_ids, curve_rows[None, :...  4.8 us
    reduce_sum x1, other arithmetic, shards(): summed = jnp.sum(lax.all_gather(in_array, 'loc'), axis=0)  2.4 us
  transfers between devices with their start and end apart: 1, of which 1 were waited for; matrix products, arithmetic and copies ran while one was open for 0% of the time, Pallas kernels for 0%

profile of v1, /device:TPU:0, one launch (start us, length us, event | category | flops | bytes accessed | tf_op | source)
XLA Modules:
  0.0 101.4 jit_solution(10905317686049293619)
XLA Ops:
  7.2 0.0 copy-start
  7.2 0.0 all-gather.2.cloned.1.call-start
  7.2 0.8 copy-done
  8.0 0.9 convolution_bitcast_fusion
  8.9 0.0 copy-start.2
  8.9 16.5 %while.11 = (s32[]{:T(128)}, f32[2,128,128]{2,1,0:T(8,128)S(1)}, f32[256]{0:T(256)}, s32[2,128,256]{2,1,0:T(8,128)}, f32[64,256]{1,0:T(8,128)S(1)}, /*index=5*/f...) while((s32[]{:T(128)}, f32[2,128,128]{2,1,0:T(8,128)S(1)}, f32[256]{0:T(256)}, ...), condition=%wide.region_3.4_spmd.clone, body=%wide.region_0.3_spmd.clone.sunk | while | flops 35602432 | bytes 1051757 | solution.py:50
  8.9 0.9 dynamic-slice_bitcast_fusion.2
  9.9 2.4 %select_reduce_fusion.2 = f32[128,256]{1,0:T(8,128)S(1)} fusion(f32[64,256]{1,0:T(8,128)S(1)} %get-tuple-element.155, s32[128,256]{1,0:T(8,128)S(1)} %dynamic-slice_bitcast_fusion.2), kind=kLoop, calls=%fused_computation.3.clone.1 | loop fusion | flops 6258688 | bytes 327680 | tf_op jit(solution)/shard_map/while/body/eval_jaxpr/reduce_sum | solution.py:41
  12.3 4.9 %minimum_reduce_fusion.2 = f32[128,128]{1,0:T(8,128)S(1)} fusion(f32[256]{0:T(256)} %get-tuple-element.158, f32[256]{0:T(256)} %get-tuple-element.157, f32[128,256]{1,0:T(8,128)} %get-tuple-element.156, f32[128,256]{1,0:T(8,128)S(1)} %select_reduce_fusion.2, f32[256]{0:T(256)} %get-tuple-element.153), kind=kLoop, calls=%fused_computation.1.clone.1 | loop fusion | flops 29343744 | bytes 330752 | tf_op jit(solution)/shard_map/while/body/eval_jaxpr/reduce_sum | solution.py:46
  17.2 0.9 dynamic-slice_bitcast_fusion.2
  18.1 2.4 %select_reduce_fusion.2 = f32[128,256]{1,0:T(8,128)S(1)} fusion(f32[64,256]{1,0:T(8,128)S(1)} %get-tuple-element.155, s32[128,256]{1,0:T(8,128)S(1)} %dynamic-slice_bitcast_fusion.2), kind=kLoop, calls=%fused_computation.3.clone.1 | loop fusion | flops 6258688 | bytes 327680 | tf_op jit(solution)/shard_map/while/body/eval_jaxpr/reduce_sum | solution.py:41
  20.5 4.9 %minimum_reduce_fusion.2 = f32[128,128]{1,0:T(8,128)S(1)} fusion(f32[256]{0:T(256)} %get-tuple-element.158, f32[256]{0:T(256)} %get-tuple-element.157, f32[128,256]{1,0:T(8,128)} %get-tuple-element.156, f32[128,256]{1,0:T(8,128)S(1)} %select_reduce_fusion.2, f32[256]{0:T(256)} %get-tuple-element.153), kind=kLoop, calls=%fused_computation.1.clone.1 | loop fusion | flops 29343744 | bytes 330752 | tf_op jit(solution)/shard_map/while/body/eval_jaxpr/reduce_sum | solution.py:46
  25.4 0.0 copy-start.1
  25.4 0.6 copy-done.1
  26.1 0.0 all-gather.2.cloned.1.call-update
  26.1 64.5 %all-gather.2.cloned.1.call-done = f32[32,256,128]{2,1,0:T(8,128)} async-done(((f32[1,256,128]{2,1,0:T(8,128)}), f32[32,256,128]{2,1,0:T(8,128)}) %all-gather.2.cloned.1.call-update) | async-done | bytes 4194320 | tf_op jit(solution)/shard_map/all_gather | solution.py:51
  90.6 2.4 %reduce_sum.27 = f32[256,128]{1,0:T(8,128)S(1)} reduce(f32[32,256,128]{2,1,0:T(8,128)} %all-gather.2.cloned.1.call-done, f32[]{:T(128)} %constant.4.clone.1), dimensions={0}, to_apply=%region_4.5 | reduce | flops 1015808 | bytes 4325380 | tf_op jit(solution)/shard_map/reduce_sum | solution.py:51
  93.0 0.0 copy-done.2
  93.0 1.0 convolution_multiply_fusion
  94.0 0.6 constant_dynamic-slice_fusion
  (4 shorter events, 0.0 us)
Async XLA Ops:
  7.2 0.8 copy-start
  7.2 83.4 %all-gather.2.cloned.1.call-start = ((), (), s32[]{:S(2)}) async-start(), calls=%async_computation | async-start | bytes 4325376 | tf_op jit(solution)/shard_map/all_gather | solution.py:51
  8.9 84.1 %copy-start.2 = (s32[256]{0:T(256)S(1)}, s32[256]{0:T(256)}, u32[]{:S(2)}) copy-start(s32[256]{0:T(256)} %param.17) | copy-start | bytes 3076
  25.4 0.6 copy-start.1
Sparse Core Ops, SparseCore 0:
  26.2 64.3 all-gather.1
